TPU v7x, 32 devices: a whole 2x2x4 slice. The times are simulated.
32 devices in a mesh: img: 2 (over x), rows: 16 (over z, y, core).
Axes of the slice: x: 2, y: 2, z: 4, core: 2. Of those that a mesh axis runs over, the one named last changes fastest.
Arguments:
- image: bfloat16 [128, 256, 512], P(('img', 'rows')), parts along dimension 0, may hold values from -32 to 32
- gain_in: float32 [512], replicated, may hold values from 0.1 to 1.9
- shift_in: float32 [512], replicated, may hold values from -3 to 3
- conv_in: bfloat16 [3, 3, 512, 512], replicated, may hold values from -0.09375 to 0.09375
- gain_mid: float32 [512], replicated, may hold values from 0.1 to 1.9
- shift_mid: float32 [512], replicated, may hold values from -3 to 3
- conv_out: bfloat16 [3, 3, 512, 512], replicated, may hold values from -0.09375 to 0.09375
- bias_out: float32 [512], replicated, may hold values from -2 to 2
Outputs:
- result: bfloat16 [128, 256, 512], P(('img', 'rows')), parts along dimension 0
There are 2 independent parts, one for each index of `img`. A program takes and returns all parts, laid end to end along the dimension named above; an argument that names none is the same for every part. Nothing has to cross between parts.
All inputs are finite; a program needn't handle non-finite values.
Results may differ from a plain program's by a relative error of at most 0.0045.
Values may be sent and summed in bfloat16 or wider, within the bound.
A program may use at most 64 MiB of HBM per device.

v0:
```python
import jax
import jax.numpy as jnp
from jax import lax
from jax.sharding import PartitionSpec as P

GROUPS = 32


def extended(block, sides, width):
    for axis, dim in sides:
        count = lax.axis_size(axis)
        forward = [(i, i + 1) for i in range(count - 1)]
        backward = [(target, source) for source, target in forward]
        low = lax.ppermute(
            lax.slice_in_dim(block, block.shape[dim] - width, None, axis=dim), axis, forward
        )
        high = lax.ppermute(lax.slice_in_dim(block, 0, width, axis=dim), axis, backward)
        block = jnp.concatenate([low, block, high], axis=dim)
    return block


def group_stats(value_entries):
    height, width, chans = value_entries.shape
    grouped = value_entries.reshape(height, width, GROUPS, chans // GROUPS)
    count = float(height * width * (chans // GROUPS) * lax.axis_size("rows"))
    sums, squares = lax.psum(
        (jnp.sum(grouped, axis=(0, 1, 3)), jnp.sum(grouped * grouped, axis=(0, 1, 3))), "rows"
    )
    midpoint_location = sums / count
    spread = squares / count - midpoint_location * midpoint_location
    return (midpoint_location, 1.0 / jnp.sqrt(spread + 1e-06))


def activate(value_entries, midpoint_location, inverse, gain, shift):
    height, width, chans = value_entries.shape
    grouped = value_entries.reshape(height, width, GROUPS, chans // GROUPS)
    scaled = ((grouped - midpoint_location[:, None]) * inverse[:, None]).reshape(
        height, width, chans
    )
    return jax.nn.silu(scaled * gain + shift).astype(jnp.bfloat16)


def conv_rows(padded_rows, kernel):
    height = padded_rows.shape[0] - 2
    width = padded_rows.shape[1]
    chans = padded_rows.shape[2]
    padded = jnp.pad(padded_rows, ((0, 0), (1, 1), (0, 0)))
    total = jnp.zeros((height * width, kernel.shape[3]), jnp.float32)
    for row_off in range(3):
        for col_off in range(3):
            window = padded[row_off : row_off + height, col_off : col_off + width].reshape(
                height * width, chans
            )
            total = total + jnp.dot(
                window, kernel[row_off, col_off], preferred_element_type=jnp.float32
            )
    return total.reshape(height, width, kernel.shape[3])


def layer(value_entries, gain, shift, kernel):
    wide = value_entries.astype(jnp.float32)
    midpoint_location, inverse = group_stats(wide)
    active = activate(wide, midpoint_location, inverse, gain, shift)
    full = extended(active, (("rows", 0),), 1)
    return conv_rows(full, kernel)


def local(image, gain_in, shift_in, conv_in, gain_mid, shift_mid, conv_out, bias_out):
    middle = layer(image, gain_in, shift_in, conv_in).astype(jnp.bfloat16)
    branch = layer(middle, gain_mid, shift_mid, conv_out)
    total = image.astype(jnp.float32) + branch + bias_out
    return total.astype(jnp.bfloat16)


def solution(mesh):
    in_specs = (P(("img", "rows"), None, None), P(), P(), P(), P(), P(), P(), P())
    out_specs = P(("img", "rows"), None, None)
    return jax.shard_map(local, mesh=mesh, in_specs=in_specs, out_specs=out_specs, check_vma=False)
```

profile of v0, /device:TPU:1, one launch (start us, length us, event | category | flops | bytes accessed | tf_op | source)
XLA Modules:
  0.0 101.8 jit_solution(5374458721862156540)
XLA Ops:
  0.0 1.6 %convert_reduce_fusion = (f32[512]{0:T(512)S(1)}, f32[512]{0:T(512)S(1)}) fusion(bf16[4,256,512]{2,1,0:T(8,128)(2,1)} %param.8), kind=kLoop, calls=%fused_computation.5 | loop fusion | flops 2096128 | bytes 1052672 | tf_op jit(solution)/shard_map/reduce_sum | solution.py:27
  1.9 30.6 %all-reduce.3 = (f32[32]{0:T(128)S(1)}, f32[32]{0:T(128)S(1)}) all-reduce(f32[32]{0:T(128)S(1)} %reduce_sum.54, f32[32]{0:T(128)S(1)} %reduce_sum.51), channel_id=1, replica_groups=mesh['img'=2,'rows'=16] {'rows'}, use_global_device_ids=true, to_apply=%region_5.6 | all-reduce | flops 64 | bytes 512 | tf_op jit(solution)/shard_map/psum | solution.py:26
  32.8 2.0 %fusion.9 = bf16[4,256,512]{2,1,0:T(8,128)(2,1)S(1)} fusion(bf16[4,256,512]{2,1,0:T(8,128)(2,1)} %param.8, f32[512]{0:T(512)} %param.10, f32[512]{0:T(512)} %param.9, f32[512]{0:T(512)S(1)} %mul.79, f32[512]{0:T(512)S(1)} %sub.38), kind=kLoop, calls=%fused_computation.15 | loop fusion | flops 5242880 | bytes 2105344 | tf_op jit(solution)/shard_map/convert_element_type | solution.py:40
  34.9 3.0 %collective-permute-start = (bf16[1,256,512]{2,1,0:T(8,128)(2,1)S(1)}, bf16[1,256,512]{2,1,0:T(8,128)(2,1)S(1)}, u32[]{:S(2)}, u32[]{:S(2)}) collective-permute-start(bf16[1,256,512]{2,1,0:T(8,128)(2,1)S(1)} %get-tuple-element.31), channel_id=1, source_target_pairs={{0,1},{1,2},{2,3},{3,4},{4,5},{5,6},{6,7},{7,8},{8,9},{9,10},{10,1... | collective-permute-start | bytes 786440 | tf_op jit(solution)/shard_map/ppermute | solution.py:14
  37.8 4.6 %collective-permute-start.1 = (bf16[1,256,512]{2,1,0:T(8,128)(2,1)S(1)}, bf16[1,256,512]{2,1,0:T(8,128)(2,1)S(1)}, u32[]{:S(2)}, u32[]{:S(2)}) collective-permute-start(bf16[1,256,512]{2,1,0:T(8,128)(2,1)S(1)} %get-tuple-element.32), channel_id=1, source_target_pairs={{1,0},{2,1},{3,2},{4,3},{5,4},{6,5},{7,6},{8,7},{9,8},{10,9},{11,1... | collective-permute-start | bytes 786440 | tf_op jit(solution)/shard_map/ppermute | solution.py:17
  42.5 1.9 %fusion.47 = f32[1024,512]{1,0:T(8,128)S(1)} fusion(bf16[1024,512]{1,0:T(8,128)(2,1)S(1)} %bitcast.93, bf16[3,3,512,512]{3,2,1,0:T(8,128)(2,1)} %param.11), kind=kOutput, calls=%fused_computation.65 | convolution fusion | flops 536870912 | bytes 3670016 | tf_op jit(solution)/shard_map/dot_general | solution.py:54
  44.4 1.1 %collective-permute-done.1 = bf16[1,256,512]{2,1,0:T(8,128)(2,1)S(1)} collective-permute-done((bf16[1,256,512]{2,1,0:T(8,128)(2,1)S(1)}, bf16[1,256,512]{2,1,0:T(8,128)(2,1)S(1)}, u32[]{:S(2)}, u32[]{:S(2)}) %collective-permute-start.1) | collective-permute-done | bytes 262176 | tf_op jit(solution)/shard_map/ppermute | solution.py:17
  46.9 0.8 fusion.77
  48.4 0.7 fusion.55
  49.1 0.7 fusion.45
  49.8 0.7 fusion.49
  50.5 0.7 fusion.51
  51.9 1.5 %convert_reduce_fusion.1 = (f32[512]{0:T(512)S(1)}, f32[512]{0:T(512)S(1)}, bf16[1024,512]{1,0:T(8,128)(2,1)S(1)}) fusion(f32[1024,512]{1,0:T(8,128)S(1)} %fusion.40, bf16[1024,512]{1,0:T(8,128)(2,1)S(1)} %bitcast.110, bf16[3,3,512,512]{3,2,1,0:T(8,128)(2,1)S(1)} %copy-done.1, f32[1024,512]{1,0:T(8,128)S(1)} %fusion.43, f32[1024,512]{1,0:T(8,128)S(1)} %fusion.45, ...), kind=kOutput, calls=%fused_computation.31 | convolution fusion | flops 543685632 | bytes 19402752 | tf_op jit(solution)/shard_map/dot_general | solution.py:54
  53.9 27.5 %all-reduce.2 = (f32[32]{0:T(128)S(1)}, f32[32]{0:T(128)S(1)}) all-reduce(f32[32]{0:T(128)S(1)} %reduce_sum.75, f32[32]{0:T(128)S(1)} %reduce_sum.72), channel_id=1, replica_groups=mesh['img'=2,'rows'=16] {'rows'}, use_global_device_ids=true, to_apply=%region_11.12 | all-reduce | flops 64 | bytes 512 | tf_op jit(solution)/shard_map/psum | solution.py:26
  81.7 0.7 multiply_convert_fusion.1
  82.5 2.2 %collective-permute-start.2 = (bf16[1,256,512]{2,1,0:T(8,128)(2,1)S(1)}, bf16[1,256,512]{2,1,0:T(8,128)(2,1)S(1)}, u32[]{:S(2)}, u32[]{:S(2)}) collective-permute-start(bf16[1,256,512]{2,1,0:T(8,128)(2,1)S(1)} %get-tuple-element.27), channel_id=1, source_target_pairs={{0,1},{1,2},{2,3},{3,4},{4,5},{5,6},{6,7},{7,8},{8,9},{9,10},{10,1... | collective-permute-start | bytes 786440 | tf_op jit(solution)/shard_map/ppermute | solution.py:14
  84.7 4.1 %collective-permute-start.3 = (bf16[1,256,512]{2,1,0:T(8,128)(2,1)S(1)}, bf16[1,256,512]{2,1,0:T(8,128)(2,1)S(1)}, u32[]{:S(2)}, u32[]{:S(2)}) collective-permute-start(bf16[1,256,512]{2,1,0:T(8,128)(2,1)S(1)} %get-tuple-element.28), channel_id=1, source_target_pairs={{1,0},{2,1},{3,2},{4,3},{5,4},{6,5},{7,6},{8,7},{9,8},{10,9},{11,1... | collective-permute-start | bytes 786440 | tf_op jit(solution)/shard_map/ppermute | solution.py:17
  88.8 2.0 %fusion.18 = f32[1024,512]{1,0:T(8,128)S(1)} fusion(bf16[1024,512]{1,0:T(8,128)(2,1)S(1)} %get-tuple-element.37, f32[512]{0:T(512)S(1)} %copy-done.3, f32[512]{0:T(512)S(1)} %copy-done.4, f32[512]{0:T(512)S(1)} %mul.88, f32[512]{0:T(512)S(1)} %sub.43, bf16[3,3,512,512]{3,2,1,0:T(8,128)(2,1)} %param.14), kind=kOutput, calls=%fused_computation.32 | convolution fusion | flops 542113792 | bytes 3678208 | tf_op jit(solution)/shard_map/dot_general | solution.py:54
  90.8 1.7 %collective-permute-done.3 = bf16[1,256,512]{2,1,0:T(8,128)(2,1)S(1)} collective-permute-done((bf16[1,256,512]{2,1,0:T(8,128)(2,1)S(1)}, bf16[1,256,512]{2,1,0:T(8,128)(2,1)S(1)}, u32[]{:S(2)}, u32[]{:S(2)}) %collective-permute-start.3) | collective-permute-done | bytes 262176 | tf_op jit(solution)/shard_map/ppermute | solution.py:17
  93.8 0.8 fusion.76
  96.1 0.7 fusion.29
  97.5 0.7 fusion.34
  98.9 1.5 %add_add_fusion = f32[1024,512]{1,0:T(8,128)S(1)} fusion(f32[1024,512]{1,0:T(8,128)S(1)} %fusion.24, f32[1024,512]{1,0:T(8,128)S(1)} %fusion.27, f32[1024,512]{1,0:T(8,128)S(1)} %fusion.29, f32[1024,512]{1,0:T(8,128)S(1)} %fusion.18, f32[1024,512]{1,0:T(8,128)S(1)} %fusion.32, f32[1024,512]{1,0:T(8,128)S(1)} %fusion.34, f32[1024,512]{1,0:T(8,128)S(1)} %fusion.38, ...), kind=kOutput, calls=%fused_computation.19 | convolution fusion | flops 541065216 | bytes 20447232 | tf_op jit(solution)/shard_map/dot_general | solution.py:54
  100.5 1.4 %fusion.12 = bf16[4,256,512]{2,1,0:T(8,128)(2,1)} fusion(f32[4,256,512]{2,1,0:T(8,128)S(1)} %bitcast.94, bf16[4,256,512]{2,1,0:T(8,128)(2,1)S(1)} %copy-done, f32[512]{0:T(512)S(1)} %copy-done.2), kind=kLoop, calls=%fused_computation.18 | loop fusion | flops 2097152 | bytes 4196352 | tf_op jit(solution)/shard_map/convert_element_type | solution.py:72
  (49 shorter events, 8.3 us)
Async XLA Ops:
  34.9 9.5 %collective-permute-start = (bf16[1,256,512]{2,1,0:T(8,128)(2,1)S(1)}, bf16[1,256,512]{2,1,0:T(8,128)(2,1)S(1)}, u32[]{:S(2)}, u32[]{:S(2)}) collective-permute-start(bf16[1,256,512]{2,1,0:T(8,128)(2,1)S(1)} %get-tuple-element.31), channel_id=1, source_target_pairs={{0,1},{1,2},{2,3},{3,4},{4,5},{5,6},{6,7},{7,8},{8,9},{9,10},{10,1... | collective-permute-start | bytes 786440 | tf_op jit(solution)/shard_map/ppermute | solution.py:14
  37.8 7.7 %collective-permute-start.1 = (bf16[1,256,512]{2,1,0:T(8,128)(2,1)S(1)}, bf16[1,256,512]{2,1,0:T(8,128)(2,1)S(1)}, u32[]{:S(2)}, u32[]{:S(2)}) collective-permute-start(bf16[1,256,512]{2,1,0:T(8,128)(2,1)S(1)} %get-tuple-element.32), channel_id=1, source_target_pairs={{1,0},{2,1},{3,2},{4,3},{5,4},{6,5},{7,6},{8,7},{9,8},{10,9},{11,1... | collective-permute-start | bytes 786440 | tf_op jit(solution)/shard_map/ppermute | solution.py:17
  42.5 3.3 %copy-start.1 = (bf16[3,3,512,512]{3,2,1,0:T(8,128)(2,1)S(1)}, bf16[3,3,512,512]{3,2,1,0:T(8,128)(2,1)}, u32[]{:S(2)}) copy-start(bf16[3,3,512,512]{3,2,1,0:T(8,128)(2,1)} %param.11) | copy-start | bytes 14155780
  51.9 29.7 %copy-start.3 = (f32[512]{0:T(512)S(1)}, f32[512]{0:T(512)}, u32[]{:S(2)}) copy-start(f32[512]{0:T(512)} %param.13) | copy-start | bytes 6148
  51.9 29.7 %copy-start.4 = (f32[512]{0:T(512)S(1)}, f32[512]{0:T(512)}, u32[]{:S(2)}) copy-start(f32[512]{0:T(512)} %param.12) | copy-start | bytes 6148
  82.4 10.3 %slice-start = ((s8[4718592]{0:T(1024)(128)(4,1)}), s8[4194304]{0:T(1024)(128)(4,1)S(1)}, s32[]{:S(2)}) async-start(s8[4718592]{0:T(1024)(128)(4,1)} %bitcast.112), calls=%async_computation | async-start | bytes 8388608
  82.5 8.3 %collective-permute-start.2 = (bf16[1,256,512]{2,1,0:T(8,128)(2,1)S(1)}, bf16[1,256,512]{2,1,0:T(8,128)(2,1)S(1)}, u32[]{:S(2)}, u32[]{:S(2)}) collective-permute-start(bf16[1,256,512]{2,1,0:T(8,128)(2,1)S(1)} %get-tuple-element.27), channel_id=1, source_target_pairs={{0,1},{1,2},{2,3},{3,4},{4,5},{5,6},{6,7},{7,8},{8,9},{9,10},{10,1... | collective-permute-start | bytes 786440 | tf_op jit(solution)/shard_map/ppermute | solution.py:14
  84.7 8.1 %slice-start.1 = ((s8[4718592]{0:T(1024)(128)(4,1)}), s8[524288]{0:T(1024)(128)(4,1)S(1)}, s32[]{:S(2)}) async-start(s8[4718592]{0:T(1024)(128)(4,1)} %bitcast.112), calls=%async_computation.1 | async-start | bytes 1048576
  84.7 7.8 %collective-permute-start.3 = (bf16[1,256,512]{2,1,0:T(8,128)(2,1)S(1)}, bf16[1,256,512]{2,1,0:T(8,128)(2,1)S(1)}, u32[]{:S(2)}, u32[]{:S(2)}) collective-permute-start(bf16[1,256,512]{2,1,0:T(8,128)(2,1)S(1)} %get-tuple-element.28), channel_id=1, source_target_pairs={{1,0},{2,1},{3,2},{4,3},{5,4},{6,5},{7,6},{8,7},{9,8},{10,9},{11,1... | collective-permute-start | bytes 786440 | tf_op jit(solution)/shard_map/ppermute | solution.py:17
  98.9 1.5 %copy-start = (bf16[4,256,512]{2,1,0:T(8,128)(2,1)S(1)}, bf16[4,256,512]{2,1,0:T(8,128)(2,1)}, u32[]{:S(2)}) copy-start(bf16[4,256,512]{2,1,0:T(8,128)(2,1)} %param.8) | copy-start | bytes 3145732
  98.9 1.5 %copy-start.2 = (f32[512]{0:T(512)S(1)}, f32[512]{0:T(512)}, u32[]{:S(2)}) copy-start(f32[512]{0:T(512)} %param.15) | copy-start | bytes 6148
where the time goes:
time: 102 us
  blocking collectives  58 us (57%)
  matrix products  16.8 us (16%)
  starting transfers between devices  13.9 us (14%)
  other arithmetic  7.29 us (7%)
  waiting for transfers between devices  2.82 us (3%)
  local copies, waits for them, and re-layouts  2.67 us (3%)
    psum x2, blocking collectives, group_stats(): lax.psum((jnp.sum(grouped, axis=(0, 1, 3)), jnp.sum(grouped * grouped, ax...  58 us
    dot_general x18, matrix products, conv_rows(): jnp.dot(window, kernel[row_off, col_off], preferred_element_type=jnp.floa...  16.8 us
    ppermute x2, starting transfers between devices, extended(): lax.ppermute(lax.slice_in_dim(block, 0, width, axis=dim), axis, backward)  8.77 us
    ppermute x2, starting transfers between devices, extended(): lax.ppermute(lax.slice_in_dim(block, block.shape[dim] - width, None, axis...  5.16 us
    ppermute x2, waiting for transfers between devices, extended(): lax.ppermute(lax.slice_in_dim(block, 0, width, axis=dim), axis, backward)  2.82 us
    convert_element_type x2, other arithmetic, activate(): return jax.nn.silu(scaled * gain + shift).astype(jnp.bfloat16)  2.7 us
  transfers between devices with their start and end apart: 4, of which 2 were waited for; matrix products, arithmetic and copies ran while one was open for 4% of the time, Pallas kernels for 0%

commit v1 on v0

v1 whole, which is shorter than its diff:
```python
import functools

import jax
import jax.numpy as jnp
from jax import lax
from jax.experimental import pallas as pl
from jax.experimental.pallas import tpu as pltpu
from jax.sharding import PartitionSpec as P

GROUPS = 32
LANES = 128
CHUNK = 32
TILE = 256
MESH = pl.DeviceIdType.MESH


def packed(sums, squares):
    chans = sums.shape[1]
    pieces = [part[:, k : k + LANES] for part in (sums, squares) for k in range(0, chans, LANES)]
    return jnp.concatenate(pieces, axis=0)


def flat(tile):
    return jnp.concatenate([tile[k : k + 1] for k in range(tile.shape[0])], axis=1)


def group_total(tile, size):
    lane = lax.broadcasted_iota(jnp.int32, tile.shape, 1)
    step = 1
    while step < size:
        up = pltpu.roll(tile, step, 1)
        down = pltpu.roll(tile, LANES - step, 1)
        tile = tile + jnp.where((lane & step) != 0, up, down)
        step *= 2
    return tile


def kernel(n, image, gain_in, shift_in, conv_in, gain_mid, shift_mid, conv_out, bias_out, out,
           img, act, mid, result, w_in, w_out, acc, gath_in, gath_mid,
           local_sem, out_sem, halo_send, halo_recv, stat_send, stat_recv):
    me = lax.axis_index("rows")
    height, width, chans = image.shape
    count = float(height * width * (chans // GROUPS) * n)
    parts = chans // LANES

    load = pltpu.make_async_copy(image, img.at[pl.ds(1, height)], local_sem.at[0])
    load.start()
    load_w_in = pltpu.make_async_copy(conv_in, w_in, local_sem.at[1])
    load_w_in.start()
    load_w_out = pltpu.make_async_copy(conv_out, w_out, local_sem.at[2])
    load_w_out.start()

    barrier = pltpu.get_barrier_semaphore()
    for d in range(1, n):
        pl.semaphore_signal(
            barrier, inc=1, device_id={"rows": lax.rem(me + d, n)}, device_id_type=MESH
        )

    def add_stats(value, lanes):
        rows = value.shape[0]
        folded = value.reshape(rows // 8, 8, value.shape[1])
        acc[0, :, lanes] += jnp.sum(folded, axis=0)
        acc[1, :, lanes] += jnp.sum(folded * folded, axis=0)

    def stat_copy(gath, which, d):
        return pltpu.make_async_remote_copy(
            src_ref=gath.at[0],
            dst_ref=gath.at[d],
            send_sem=stat_send.at[which, d],
            recv_sem=stat_recv.at[which, d],
            device_id={"rows": lax.rem(me + d, n)},
            device_id_type=MESH,
        )

    def send_stats(gath, which):
        sums = jnp.sum(acc[0], axis=0, keepdims=True)
        squares = jnp.sum(acc[1], axis=0, keepdims=True)
        gath[0] = packed(sums, squares)
        for d in range(1, n):
            stat_copy(gath, which, d).start()

    def receive_stats(gath, which, gain):
        for d in range(1, n):
            stat_copy(gath, which, d).wait()
        total = group_total(jnp.sum(gath[...], axis=0), chans // GROUPS) / count
        mean, square = total[:parts], total[parts:]
        variance = jnp.maximum(square - mean * mean, 0.0)
        return flat(mean), flat(lax.rsqrt(variance + 1e-06)) * gain[...]

    def halo_copies(buf, which):
        up = pltpu.make_async_remote_copy(
            src_ref=buf.at[1],
            dst_ref=buf.at[height + 1],
            send_sem=halo_send.at[which, 0],
            recv_sem=halo_recv.at[which, 0],
            device_id={"rows": jnp.maximum(me - 1, 0)},
            device_id_type=MESH,
        )
        down = pltpu.make_async_remote_copy(
            src_ref=buf.at[height],
            dst_ref=buf.at[0],
            send_sem=halo_send.at[which, 1],
            recv_sem=halo_recv.at[which, 1],
            device_id={"rows": jnp.minimum(me + 1, n - 1)},
            device_id_type=MESH,
        )
        return up, down

    def send_halo(buf, which):
        up, down = halo_copies(buf, which)

        @pl.when(me > 0)
        def _():
            up.start()

        @pl.when(me < n - 1)
        def _():
            down.start()

    def activate(buf, row, mean, scale, shift):
        def step(k, _):
            cols = pl.ds(pl.multiple_of(k * CHUNK, CHUNK), CHUNK)
            half = 0.5 * ((buf[row, cols].astype(jnp.float32) - mean) * scale + shift)
            act[row, cols] = (half + half * jnp.tanh(half)).astype(jnp.bfloat16)
            return 0

        lax.fori_loop(0, width // CHUNK, step, 0, unroll=2)

    def activate_halo(buf, which, mean, scale, shift):
        up, down = halo_copies(buf, which)

        @pl.when(me > 0)
        def _():
            up.wait_send()
            down.wait_recv()
            activate(buf, 0, mean, scale, shift)

        @pl.when(me == 0)
        def _():
            act[0] = jnp.zeros((width, chans), jnp.bfloat16)

        @pl.when(me < n - 1)
        def _():
            down.wait_send()
            up.wait_recv()
            activate(buf, height + 1, mean, scale, shift)

        @pl.when(me == n - 1)
        def _():
            act[height + 1] = jnp.zeros((width, chans), jnp.bfloat16)

    def convolve(rows, weights, finish):
        def step(t, _):
            lanes = pl.ds(pl.multiple_of(t * TILE, TILE), TILE)
            left = jnp.concatenate(
                [jnp.concatenate([act[r + i] for i in range(3)], axis=1) for r in rows], axis=0
            )
            size = left.shape[0]
            y = [
                jnp.dot(
                    left,
                    weights[:, j, :, lanes].reshape(3 * chans, TILE),
                    preferred_element_type=jnp.float32,
                )
                for j in range(3)
            ]
            col = lax.rem(lax.broadcasted_iota(jnp.int32, (size, TILE), 0), width)
            total = y[1] + jnp.where(col == 0, 0.0, pltpu.roll(y[0], 1, 0))
            total = total + jnp.where(col == width - 1, 0.0, pltpu.roll(y[2], size - 1, 0))
            finish(total, lanes)
            return 0

        lax.fori_loop(0, chans // TILE, step, 0)

    acc[...] = jnp.zeros_like(acc)
    load.wait()

    def stats_step(k, _):
        cols = pl.ds(pl.multiple_of(k * CHUNK, CHUNK), CHUNK)
        for r in range(height):
            add_stats(img[1 + r, cols].astype(jnp.float32), slice(None))
        return 0

    lax.fori_loop(0, width // CHUNK, stats_step, 0)
    pl.semaphore_wait(barrier, n - 1)
    send_stats(gath_in, 0)
    send_halo(img, 0)
    acc[...] = jnp.zeros_like(acc)

    inner = [(r, r + 1) for r in range(1, height - 1, 2)]
    outer = (0, height - 1)

    mean, scale = receive_stats(gath_in, 0, gain_in)
    shift = shift_in[...]
    for r in range(1, height + 1):
        activate(img, r, mean, scale, shift)
    load_w_in.wait()

    def keep(rows):
        def finish(total, lanes):
            value = total.astype(jnp.bfloat16)
            add_stats(value.astype(jnp.float32), lanes)
            for k, r in enumerate(rows):
                mid[1 + r, :, lanes] = value[k * width : (k + 1) * width]
        return finish

    for rows in inner:
        convolve(rows, w_in, keep(rows))
    activate_halo(img, 0, mean, scale, shift)
    convolve(outer, w_in, keep(outer))

    send_stats(gath_mid, 1)
    send_halo(mid, 1)
    mean, scale = receive_stats(gath_mid, 1, gain_mid)
    shift = shift_mid[...]
    for r in range(1, height + 1):
        activate(mid, r, mean, scale, shift)
    load_w_out.wait()

    def give(rows):
        def finish(total, lanes):
            bias = bias_out[:, lanes]
            for k, r in enumerate(rows):
                piece = total[k * width : (k + 1) * width] + bias
                piece = img[1 + r, :, lanes].astype(jnp.float32) + piece
                result[r, :, lanes] = piece.astype(jnp.bfloat16)
        return finish

    def store(r):
        return pltpu.make_async_copy(result.at[r], out.at[r], out_sem.at[r])

    for rows in inner:
        convolve(rows, w_out, give(rows))
        for r in rows:
            store(r).start()
    activate_halo(mid, 1, mean, scale, shift)
    convolve(outer, w_out, give(outer))
    for r in outer:
        store(r).start()
    for r in range(height):
        store(r).wait()


def local(n, image, gain_in, shift_in, conv_in, gain_mid, shift_mid, conv_out, bias_out):
    height, width, chans = image.shape
    whole = pl.BlockSpec(memory_space=pl.ANY)
    vector = pl.BlockSpec(memory_space=pltpu.VMEM)
    bf16, f32 = jnp.bfloat16, jnp.float32
    rows = 2 * chans // LANES
    return pl.pallas_call(
        functools.partial(kernel, n),
        out_shape=jax.ShapeDtypeStruct(image.shape, image.dtype),
        in_specs=[whole, vector, vector, whole, vector, vector, whole, vector],
        out_specs=whole,
        scratch_shapes=[
            pltpu.VMEM((height + 2, width, chans), bf16),
            pltpu.VMEM((height + 2, width, chans), bf16),
            pltpu.VMEM((height + 2, width, chans), bf16),
            pltpu.VMEM((height, width, chans), bf16),
            pltpu.VMEM(conv_in.shape, bf16),
            pltpu.VMEM(conv_out.shape, bf16),
            pltpu.VMEM((2, 8, chans), f32),
            pltpu.VMEM((n, rows, LANES), f32),
            pltpu.VMEM((n, rows, LANES), f32),
            pltpu.SemaphoreType.DMA((3,)),
            pltpu.SemaphoreType.DMA((height,)),
            pltpu.SemaphoreType.DMA((2, 2)),
            pltpu.SemaphoreType.DMA((2, 2)),
            pltpu.SemaphoreType.DMA((2, n)),
            pltpu.SemaphoreType.DMA((2, n)),
        ],
        compiler_params=pltpu.CompilerParams(
            collective_id=0, has_side_effects=True, vmem_limit_bytes=60 * 1024 * 1024
        ),
    )(image, gain_in[None], shift_in[None], conv_in, gain_mid[None], shift_mid[None], conv_out,
      bias_out[None])


def solution(mesh):
    n = mesh.shape["rows"]
    in_specs = (P(("img", "rows"), None, None), P(), P(), P(), P(), P(), P(), P())
    out_specs = P(("img", "rows"), None, None)
    return jax.shard_map(
        functools.partial(local, n), mesh=mesh, in_specs=in_specs, out_specs=out_specs,
        check_vma=False,
    )
```

time: 102 us -> 33.4 us (0.33)
  blocking collectives: 58 us -> 0 us
  Pallas kernels: 0 us -> 30.7 us
  matrix products: 16.8 us -> 0 us
  starting transfers between devices: 13.9 us -> 0 us
  other arithmetic: 7.29 us -> 0 us
  waiting for transfers between devices: 2.82 us -> 0 us
    psum x2 -> x0, blocking collectives: 58 us -> none  [group_stats(): lax.psum((jnp.sum(grouped, axis=(0, 1, 3)), jnp.sum(grouped * grouped, ax...]
    pallas_call x0 -> x1, Pallas kernels: none -> 30.7 us  [local(): pl.pallas_call(functools.partial(kernel, n), out_shape=jax.ShapeDtypeStru...]
    dot_general x18 -> x0, matrix products: 16.8 us -> none  [conv_rows(): jnp.dot(window, kernel[row_off, col_off], preferred_element_type=jnp.floa...]
    ppermute x4 -> x0, starting transfers between devices: 13.9 us -> none  [the longest x2 8.77 us: extended(): lax.ppermute(lax.slice_in_dim(block, 0, width, axis=dim), axis, backward)]
    convert_element_type x3 -> x0, other arithmetic: 4.06 us -> none  [the longest x2 2.7 us: activate(): return jax.nn.silu(scaled * gain + shift).astype(jnp.bfloat16)]
    ppermute x4 -> x0, waiting for transfers between devices: 2.82 us -> none  [the longest x2 2.82 us: extended(): lax.ppermute(lax.slice_in_dim(block, 0, width, axis=dim), axis, backward)]
    unnamed x14 -> x1, local copies, waits for them, and re-layouts: 0.05 us -> 2.26 us
    reduce_sum x5 -> x0, other arithmetic: 2.02 us -> none  [the longest x3 1.79 us: group_stats(): jnp.sum(grouped, axis=(0, 1, 3))]
  transfers between devices with their start and end apart: 4 -> 0, of which waited for: 2 -> 0; matrix products, arithmetic and copies ran while one was open for 4% -> 0% of each run, Pallas kernels for 0% -> 0%
where the time goes in v1:
time: 33.4 us; the launch traced here: 32.9 us
  Pallas kernels  30.7 us (92%)
  local copies, waits for them, and re-layouts  2.26 us (7%)
    pallas_call x1, Pallas kernels, local(): pl.pallas_call(functools.partial(kernel, n), out_shape=jax.ShapeDtypeStru...  30.7 us
    unnamed x1, local copies, waits for them, and re-layouts  2.26 us

profile of v1, /device:TPU:1, one launch (start us, length us, event | category | flops | bytes accessed | tf_op | source)
XLA Modules:
  0.0 32.9 jit_solution(10415079470039976945)
XLA Ops:
  0.0 30.7 %shard_map.82 = bf16[4,256,512]{2,1,0:T(8,128)(2,1)} custom-call(bf16[4,256,512]{2,1,0:T(8,128)(2,1)} %image.1, f32[1,512]{1,0:T(1,128)} %bitcast.5, f32[1,512]{1,0:T(1,128)} %bitcast.6, bf16[3,3,512,512]{3,2,1,0:T(8,128)(2,1)} %conv_in.1, f32[1,512]{1,0:T(1,128)} %bitcast.7, f32[1,512]{1,0:T(1,128)} %bitcast.8, bf16[3,3,512,512]{3,2,1,0:T(8,128)(2,1)} %conv_out.1, ...), custom_call_target="tpu_custom_call" | custom-call | tf_op jit(solution)/shard_map/pallas_call | solution.py:250
  30.7 2.3 %copy.10 = bf16[4,256,512]{2,1,0:T(8,128)(2,1)} copy(bf16[4,256,512]{2,1,0:T(8,128)(2,1)} %shard_map.82) | data formatting | bytes 2097152

commit v2 on v1

--- a/solution.py
+++ b/solution.py
@@ -36,7 +36,7 @@
 
 
 def kernel(n, image, gain_in, shift_in, conv_in, gain_mid, shift_mid, conv_out, bias_out, out,
-           img, act, mid, result, w_in, w_out, acc, gath_in, gath_mid,
+           img, act, mid, result, w_in, w_out, w_mix, v_mix, acc, gath_in, gath_mid,
            local_sem, out_sem, halo_send, halo_recv, stat_send, stat_recv):
     me = lax.axis_index("rows")
     height, width, chans = image.shape
@@ -85,7 +85,7 @@
         total = group_total(jnp.sum(gath[...], axis=0), chans // GROUPS) / count
         mean, square = total[:parts], total[parts:]
         variance = jnp.maximum(square - mean * mean, 0.0)
-        return flat(mean), flat(lax.rsqrt(variance + 1e-06)) * gain[...]
+        return flat(mean), flat(lax.rsqrt(variance + 1e-06)) * (0.5 * gain[...])
 
     def halo_copies(buf, which):
         up = pltpu.make_async_remote_copy(
@@ -120,7 +120,7 @@
     def activate(buf, row, mean, scale, shift):
         def step(k, _):
             cols = pl.ds(pl.multiple_of(k * CHUNK, CHUNK), CHUNK)
-            half = 0.5 * ((buf[row, cols].astype(jnp.float32) - mean) * scale + shift)
+            half = (buf[row, cols].astype(jnp.float32) - mean) * scale + shift
             act[row, cols] = (half + half * jnp.tanh(half)).astype(jnp.bfloat16)
             return 0
 
@@ -148,6 +148,54 @@
         @pl.when(me == n - 1)
         def _():
             act[height + 1] = jnp.zeros((width, chans), jnp.bfloat16)
+
+    def combine(y):
+        size = y[0].shape[0]
+        col = lax.rem(lax.broadcasted_iota(jnp.int32, y[0].shape, 0), width)
+        total = y[1] + jnp.where(col == 0, 0.0, pltpu.roll(y[0], 1, 0))
+        return total + jnp.where(col == width - 1, 0.0, pltpu.roll(y[2], size - 1, 0))
+
+    def mix_weights():
+        def step(k, _):
+            taps = pl.ds(pl.multiple_of(k * CHUNK, CHUNK), CHUNK)
+            for j in range(3):
+                ends = 0.5 * (
+                    w_out[0, j, taps].astype(jnp.float32) + w_out[2, j, taps].astype(jnp.float32)
+                )
+                centre = 0.5 * w_out[1, j, taps].astype(jnp.float32)
+                w_mix[0, j, taps] = (ends + centre).astype(jnp.bfloat16)
+                w_mix[1, j, taps] = (ends - centre).astype(jnp.bfloat16)
+            return 0
+
+        lax.fori_loop(0, chans // CHUNK, step, 0)
+
+    def convolve_pair(row, finish):
+        def mix(k, _):
+            cols = pl.ds(pl.multiple_of(k * CHUNK, CHUNK), CHUNK)
+            d = [act[row + i, cols].astype(jnp.float32) for i in range(4)]
+            for i, value in enumerate((d[0] - d[2], d[1] + d[2], d[2] - d[1], d[1] - d[3])):
+                v_mix[i, cols] = value.astype(jnp.bfloat16)
+            return 0
+
+        lax.fori_loop(0, width // CHUNK, mix, 0, unroll=2)
+
+        def step(t, _):
+            lanes = pl.ds(pl.multiple_of(t * TILE, TILE), TILE)
+            taps = (w_out.at[0], w_mix.at[0], w_mix.at[1], w_out.at[2])
+            y = [
+                [
+                    jnp.dot(v_mix[i], taps[i][j, :, lanes], preferred_element_type=jnp.float32)
+                    for j in range(3)
+                ]
+                for i in range(4)
+            ]
+            part = [combine(products) for products in y]
+            first = part[0] + (part[1] + part[2])
+            second = (part[1] - part[2]) - part[3]
+            finish(jnp.concatenate([first, second], axis=0), lanes)
+            return 0
+
+        lax.fori_loop(0, chans // TILE, step, 0)
 
     def convolve(rows, weights, finish):
         def step(t, _):
@@ -155,7 +203,6 @@
             left = jnp.concatenate(
                 [jnp.concatenate([act[r + i] for i in range(3)], axis=1) for r in rows], axis=0
             )
-            size = left.shape[0]
             y = [
                 jnp.dot(
                     left,
@@ -164,9 +211,7 @@
                 )
                 for j in range(3)
             ]
-            col = lax.rem(lax.broadcasted_iota(jnp.int32, (size, TILE), 0), width)
-            total = y[1] + jnp.where(col == 0, 0.0, pltpu.roll(y[0], 1, 0))
-            total = total + jnp.where(col == width - 1, 0.0, pltpu.roll(y[2], size - 1, 0))
+            total = combine(y)
             finish(total, lanes)
             return 0
 
@@ -190,8 +235,10 @@
     inner = [(r, r + 1) for r in range(1, height - 1, 2)]
     outer = (0, height - 1)
 
+    load_w_out.wait()
+    mix_weights()
     mean, scale = receive_stats(gath_in, 0, gain_in)
-    shift = shift_in[...]
+    shift = 0.5 * shift_in[...]
     for r in range(1, height + 1):
         activate(img, r, mean, scale, shift)
     load_w_in.wait()
@@ -212,10 +259,9 @@
     send_stats(gath_mid, 1)
     send_halo(mid, 1)
     mean, scale = receive_stats(gath_mid, 1, gain_mid)
-    shift = shift_mid[...]
+    shift = 0.5 * shift_mid[...]
     for r in range(1, height + 1):
         activate(mid, r, mean, scale, shift)
-    load_w_out.wait()
 
     def give(rows):
         def finish(total, lanes):
@@ -230,7 +276,7 @@
         return pltpu.make_async_copy(result.at[r], out.at[r], out_sem.at[r])
 
     for rows in inner:
-        convolve(rows, w_out, give(rows))
+        convolve_pair(rows[0], give(rows))
         for r in rows:
             store(r).start()
     activate_halo(mid, 1, mean, scale, shift)
@@ -259,6 +305,8 @@
             pltpu.VMEM((height, width, chans), bf16),
             pltpu.VMEM(conv_in.shape, bf16),
             pltpu.VMEM(conv_out.shape, bf16),
+            pltpu.VMEM((2,) + conv_out.shape[1:], bf16),
+            pltpu.VMEM((4, width, chans), bf16),
             pltpu.VMEM((2, 8, chans), f32),
             pltpu.VMEM((n, rows, LANES), f32),
             pltpu.VMEM((n, rows, LANES), f32),

time: 33.4 us -> 32.5 us (0.973)
  Pallas kernels: 30.7 us -> 29.7 us
    pallas_call x1, Pallas kernels: 30.7 us -> 29.7 us  [local(): pl.pallas_call(functools.partial(kernel, n), out_shape=jax.ShapeDtypeStru...]
where the time goes in v2:
time: 32.5 us; the launch traced here: 32 us
  Pallas kernels  29.7 us (91%)
  local copies, waits for them, and re-layouts  2.26 us (7%)
    pallas_call x1, Pallas kernels, local(): pl.pallas_call(functools.partial(kernel, n), out_shape=jax.ShapeDtypeStru...  29.7 us
    unnamed x1, local copies, waits for them, and re-layouts  2.26 us

profile of v2, /device:TPU:1, one launch (start us, length us, event | category | flops | bytes accessed | tf_op | source)
XLA Modules:
  0.0 32.0 jit_solution(12160278230509236025)
XLA Ops:
  0.0 29.7 %shard_map.82 = bf16[4,256,512]{2,1,0:T(8,128)(2,1)} custom-call(bf16[4,256,512]{2,1,0:T(8,128)(2,1)} %image.1, f32[1,512]{1,0:T(1,128)} %bitcast.5, f32[1,512]{1,0:T(1,128)} %bitcast.6, bf16[3,3,512,512]{3,2,1,0:T(8,128)(2,1)} %conv_in.1, f32[1,512]{1,0:T(1,128)} %bitcast.7, f32[1,512]{1,0:T(1,128)} %bitcast.8, bf16[3,3,512,512]{3,2,1,0:T(8,128)(2,1)} %conv_out.1, ...), custom_call_target="tpu_custom_call" | custom-call | tf_op jit(solution)/shard_map/pallas_call | solution.py:296
  29.7 2.3 %copy.10 = bf16[4,256,512]{2,1,0:T(8,128)(2,1)} copy(bf16[4,256,512]{2,1,0:T(8,128)(2,1)} %shard_map.82) | data formatting | bytes 2097152
